TPU v7x, 32 devices: a whole 2x2x4 slice. The times are simulated.
32 devices in a mesh: dp: 4 (over z), row: 4 (over y, core), col: 2 (over x).
Axes of the slice: x: 2, y: 2, z: 4, core: 2. Of those that a mesh axis runs over, the one named last changes fastest.
Arguments:
- inputs: bfloat16 [16384, 1024], P(('dp', 'col'), 'row'), may hold values from -6 to 6
- gain_first: float32 [1024], P('row'), may hold values from 0.5 to 1.5
- shift_first: float32 [1024], P('row'), may hold values from -1 to 1
- w_query: bfloat16 [1024, 1024], P('row', 'col'), may hold values from -0.1875 to 0.1875
- w_key: bfloat16 [1024, 1024], P('row', 'col'), may hold values from -0.1875 to 0.1875
- w_value: bfloat16 [1024, 1024], P('row', 'col'), may hold values from -0.1875 to 0.1875
- w_output: bfloat16 [1024, 1024], P('col', 'row'), may hold values from -1.5 to 1.5
- gain_second: float32 [1024], P('row'), may hold values from 0.5 to 1.5
- shift_second: float32 [1024], P('row'), may hold values from -1 to 1
- w_up: bfloat16 [1024, 4096], P('row', 'col'), may hold values from -0.1875 to 0.1875
- bias_up: float32 [4096], P('col'), may hold values from -1.5 to 1.5
- w_down: bfloat16 [4096, 1024], P('col', 'row'), may hold values from -0.09375 to 0.09375
- bias_down: float32 [1024], P('row'), may hold values from -2.5 to 2.5
- segments: int32 [16, 1024], P(('dp', 'row')), may hold values from 0 to 4, as said below
- random_blocks: int32 [16, 16, 3], P('col'), may hold values from 0 to 15
- global_blocks: int32 [2], replicated, may hold values from 0 to 15, as said below
- cotangent: bfloat16 [16384, 1024], P(('dp', 'col'), 'row'), may hold values from -6 to 6
Outputs:
- layer_out: bfloat16 [16384, 1024], P(('dp', 'col'), 'row')
- grad_inputs: float32 [16384, 1024], P(('dp', 'col'), 'row')
- grad_gain_first: float32 [1024], P('row')
- grad_shift_first: float32 [1024], P('row')
- grad_w_query: float32 [1024, 1024], P('row', 'col')
- grad_w_key: float32 [1024, 1024], P('row', 'col')
- grad_w_value: float32 [1024, 1024], P('row', 'col')
- grad_w_output: float32 [1024, 1024], P('col', 'row')
- grad_gain_second: float32 [1024], P('row')
- grad_shift_second: float32 [1024], P('row')
- grad_w_up: float32 [1024, 4096], P('row', 'col')
- grad_bias_up: float32 [4096], P('col')
- grad_w_down: float32 [4096, 1024], P('col', 'row')
- grad_bias_down: float32 [1024], P('row')
Inputs may be any that keep to these rules, and one draw needn't show every extreme that they name: `segments`: each sequence of 1024 tokens holds four documents labelled 1, 2, 3, 4 in order, then 1 to 64 padding tokens labelled 0; each of the first three documents has 100 to 300 tokens. `global_blocks`: distinct block positions; one of them is the last block, 15.
All inputs are finite; a program needn't handle non-finite values.
Results may differ from a plain program's by a relative error of at most 0.015.
Values may be sent and summed in bfloat16 or wider, within the bound.
No kernel may reach another device: no remote copies, remote signals or barrier semaphores. Data moves between devices by JAX's collectives and lax.ppermute only.
A program may use at most 256 MiB of HBM per device.

v0:
```python
import math
import jax
import jax.numpy as jnp
from jax import lax
from jax.sharding import PartitionSpec as P

D = 1024
HD = 64
BLK = 64
NB = 16
EPS = 1e-05


def product(picked, weight, flipped):
    if flipped:
        return lax.dot_general(
            picked, weight, (((1,), (1,)), ((), ())), preferred_element_type=jnp.float32
        )
    return jnp.dot(picked, weight, preferred_element_type=jnp.float32)


def to_columns(moving, weight, flipped):
    gathered = lax.all_gather(moving, "col", axis=0, tiled=True)
    row_count = gathered.shape[0] // lax.axis_size("row")

    def term_rows(first_row, how_many):
        return product(gathered, weight, flipped)

    result = lax.psum_scatter(
        term_rows(jnp.int32(0), lax.axis_size("row") * row_count),
        "row",
        scatter_dimension=0,
        tiled=True,
    )
    return (result, gathered)


def to_rows(moving, weight, flipped):
    gathered = lax.all_gather(moving, "row", axis=0, tiled=True)
    row_count = gathered.shape[0] // lax.axis_size("col")

    def term_rows(first_row, how_many):
        return product(gathered, weight, flipped)

    return (
        lax.psum_scatter(
            term_rows(jnp.int32(0), lax.axis_size("col") * row_count),
            "col",
            scatter_dimension=0,
            tiled=True,
        ),
        gathered,
    )


def norm_sums(first_sum, second_sum):
    return lax.psum((first_sum, second_sum), "row")


def norm_forward(moving, gain_row, shift_row):
    totals, squares = norm_sums(jnp.sum(moving, axis=1), jnp.sum(moving * moving, axis=1))
    center = totals / D
    spread = squares / D - center * center
    inverse = lax.rsqrt(spread + EPS)
    normed = (moving - center[:, None]) * inverse[:, None]
    return (normed * gain_row + shift_row, normed, inverse)


def norm_backward(upstream, normed, inverse, gain_row):
    scaled = upstream * gain_row
    first_sum, second_sum = norm_sums(jnp.sum(scaled, axis=1), jnp.sum(scaled * normed, axis=1))
    return inverse[:, None] * (scaled - first_sum[:, None] / D - normed * (second_sum[:, None] / D))


def head_masks(random_blocks, global_blocks):
    block_ids = jnp.arange(NB, dtype=jnp.int32)
    nearby = jnp.abs(block_ids[:, None] - block_ids[None, :]) <= 1
    chosen = jnp.any(random_blocks[:, :, :, None] == block_ids[None, None, None, :], axis=2)
    marked = jnp.any(global_blocks[:, None] == block_ids[None, :], axis=0)
    block_table = nearby[None] | chosen | marked[None, None, :] | marked[None, :, None]
    return jnp.repeat(jnp.repeat(block_table, BLK, axis=1), BLK, axis=2)


def seq_logits(seq_queries, seq_keys, labels, pattern):
    same_doc = (labels[:, None] == labels[None, :]) & (labels[None, :] != 0)
    raw_scores = jnp.einsum(
        "qhd,khd->hqk", seq_queries, seq_keys, preferred_element_type=jnp.float32
    )
    return jnp.where(pattern & same_doc[None], raw_scores * (1.0 / math.sqrt(HD)), -1000000000.0)


def attend_forward(queries, key_block, value_block, segments, pattern):

    def one_seq(pieces):
        seq_queries, seq_keys, seq_values, labels = pieces
        logits = seq_logits(seq_queries, seq_keys, labels, pattern)
        row_peak = jnp.max(logits, axis=2, keepdims=True)
        exp_terms = jnp.exp(logits - row_peak)
        row_total = jnp.sum(exp_terms, axis=2, keepdims=True)
        softmax = (exp_terms / row_total).astype(jnp.bfloat16)
        attended = jnp.einsum(
            "hqk,khd->qhd", softmax, seq_values, preferred_element_type=jnp.float32
        )
        live_rows = (labels != 0).astype(jnp.float32)
        return (attended * live_rows[:, None, None], (row_peak + jnp.log(row_total))[:, :, 0])

    return lax.map(one_seq, (queries, key_block, value_block, segments))


def attend_backward(queries, key_block, value_block, segments, pattern, grad_heads, log_total):

    def one_seq(pieces):
        seq_queries, seq_keys, seq_values, labels, seq_grads, seq_log = pieces
        logits = seq_logits(seq_queries, seq_keys, labels, pattern)
        softmax = jnp.exp(logits - seq_log[:, :, None])
        grad_probs = jnp.einsum(
            "qhd,khd->hqk", seq_grads, seq_values, preferred_element_type=jnp.float32
        )
        grad_values = jnp.einsum(
            "hqk,qhd->khd",
            softmax.astype(jnp.bfloat16),
            seq_grads,
            preferred_element_type=jnp.float32,
        )
        inner_sum = jnp.sum(softmax * grad_probs, axis=2, keepdims=True)
        grad_raw = (softmax * (grad_probs - inner_sum) * (1.0 / math.sqrt(HD))).astype(jnp.bfloat16)
        grad_queries = jnp.einsum(
            "hqk,khd->qhd", grad_raw, seq_keys, preferred_element_type=jnp.float32
        )
        grad_keys = jnp.einsum(
            "hqk,qhd->khd", grad_raw, seq_queries, preferred_element_type=jnp.float32
        )
        return (grad_queries, grad_keys, grad_values)

    return lax.map(one_seq, (queries, key_block, value_block, segments, grad_heads, log_total))


def gelu_tanh(values):
    return jax.nn.gelu(values, approximate=True)


def weight_grad(left, right):
    return lax.dot_general(
        left, right, (((0,), (0,)), ((), ())), preferred_element_type=jnp.float32
    )


def body(
    inputs,
    gain_first,
    shift_first,
    w_query,
    w_key,
    w_value,
    w_output,
    gain_second,
    shift_second,
    w_up,
    bias_up,
    w_down,
    bias_down,
    segments,
    random_blocks,
    global_blocks,
    cotangent,
):
    seq_count, seq_len = segments.shape
    head_width = w_query.shape[1]
    heads_here = random_blocks.shape[0]
    seq_shape = (seq_count, seq_len, heads_here, HD)
    pattern = head_masks(random_blocks, global_blocks)
    live_tokens = (segments != 0).reshape(-1)
    x_first = inputs.astype(jnp.float32)
    first_full, normed_one, inverse_one = norm_forward(x_first, gain_first, shift_first)
    first_low = first_full.astype(jnp.bfloat16)
    stacked = jnp.concatenate((w_query, w_key, w_value), axis=1)
    projected, first_all = to_columns(first_low, stacked, False)
    proj_low = projected.astype(jnp.bfloat16)
    queries = proj_low[:, :head_width].reshape(seq_shape)
    key_block = proj_low[:, head_width : 2 * head_width].reshape(seq_shape)
    value_block = proj_low[:, 2 * head_width :].reshape(seq_shape)
    heads_out, log_total = attend_forward(queries, key_block, value_block, segments, pattern)
    heads_low = heads_out.reshape(-1, head_width).astype(jnp.bfloat16)
    mixed_out, heads_all = to_rows(heads_low, w_output, False)
    residual = x_first + mixed_out
    second_full, normed_two, inverse_two = norm_forward(residual, gain_second, shift_second)
    second_low = second_full.astype(jnp.bfloat16)
    upward, second_all = to_columns(second_low, w_up, False)
    upward = upward + bias_up
    hidden_low = gelu_tanh(upward).astype(jnp.bfloat16)
    downward, hidden_all = to_rows(hidden_low, w_down, False)
    layer_out = (residual + (downward + bias_down)).astype(jnp.bfloat16)
    grad_hidden, cotangent_all = to_columns(cotangent, w_down, True)
    activated, pull_back = jax.vjp(gelu_tanh, upward)
    grad_upward = pull_back(grad_hidden)[0].astype(jnp.bfloat16)
    grad_second, grad_upward_all = to_rows(grad_upward, w_up, True)
    grad_residual = cotangent.astype(jnp.float32) + norm_backward(
        grad_second, normed_two, inverse_two, gain_second
    )
    grad_mixed = grad_residual.astype(jnp.bfloat16)
    grad_heads, grad_mixed_all = to_columns(grad_mixed, w_output, True)
    grad_heads = jnp.where(live_tokens[:, None], grad_heads, 0.0).astype(jnp.bfloat16)
    grad_queries, grad_keys, grad_values = attend_backward(
        queries, key_block, value_block, segments, pattern, grad_heads.reshape(seq_shape), log_total
    )
    grad_proj = jnp.concatenate(
        (
            grad_queries.reshape(-1, head_width),
            grad_keys.reshape(-1, head_width),
            grad_values.reshape(-1, head_width),
        ),
        axis=1,
    ).astype(jnp.bfloat16)
    grad_first, grad_proj_all = to_rows(grad_proj, stacked, True)
    grad_inputs = grad_residual + norm_backward(grad_first, normed_one, inverse_one, gain_first)
    grad_stacked = weight_grad(first_all, grad_proj_all)
    grad_out_weight = weight_grad(heads_all, grad_mixed_all)
    grad_up_weight = weight_grad(second_all, grad_upward_all)
    grad_down_weight = weight_grad(hidden_all, cotangent_all)
    grad_up_bias = jnp.sum(grad_upward_all, axis=0, dtype=jnp.float32)
    grad_down_bias = jnp.sum(cotangent_all, axis=0, dtype=jnp.float32)
    gain_terms = lax.psum(
        (
            jnp.sum(grad_first * normed_one, axis=0),
            jnp.sum(grad_first, axis=0),
            jnp.sum(grad_second * normed_two, axis=0),
            jnp.sum(grad_second, axis=0),
        ),
        ("dp", "col"),
    )
    summed = (
        lax.psum(grad_stacked.astype(jnp.bfloat16), "dp").astype(jnp.float32),
        lax.psum(grad_out_weight.astype(jnp.bfloat16), "dp").astype(jnp.float32),
        lax.psum(grad_up_weight.astype(jnp.bfloat16), "dp").astype(jnp.float32),
        lax.psum(grad_down_weight.astype(jnp.bfloat16), "dp").astype(jnp.float32),
        lax.psum(grad_up_bias.astype(jnp.bfloat16), "dp").astype(jnp.float32),
        lax.psum(grad_down_bias.astype(jnp.bfloat16), "dp").astype(jnp.float32),
    )
    return (
        layer_out,
        grad_inputs,
        gain_terms[0],
        gain_terms[1],
        summed[0][:, :head_width],
        summed[0][:, head_width : 2 * head_width],
        summed[0][:, 2 * head_width :],
        summed[1],
        gain_terms[2],
        gain_terms[3],
        summed[2],
        summed[4],
        summed[3],
        summed[5],
    )


def solution(mesh):
    placed = (
        P(("dp", "col"), "row"),
        P("row"),
        P("row"),
        P("row", "col"),
        P("row", "col"),
        P("row", "col"),
        P("col", "row"),
        P("row"),
        P("row"),
        P("row", "col"),
        P("col"),
        P("col", "row"),
        P("row"),
        P(("dp", "row"), None),
        P("col", None, None),
        P(),
        P(("dp", "col"), "row"),
    )
    return jax.shard_map(
        body,
        mesh=mesh,
        in_specs=placed,
        out_specs=(
            P(("dp", "col"), "row"),
            P(("dp", "col"), "row"),
            P("row"),
            P("row"),
            P("row", "col"),
            P("row", "col"),
            P("row", "col"),
            P("col", "row"),
            P("row"),
            P("row"),
            P("row", "col"),
            P("col"),
            P("col", "row"),
            P("row"),
        ),
        check_vma=False,
    )
```

profile of v0, /device:TPU:0, one launch (start us, length us, event | category | flops | bytes accessed | tf_op | source)
XLA Modules:
  0.0 1793.3 jit_solution(9766734146856281676)
XLA Ops:
  7.3 2.0 convert_reduce_fusion
  9.2 12.7 all-reduce.4
  22.6 2.5 fusion.36
  25.3 33.4 %all-gather.9.cloned.1.call-done = bf16[4096,256]{1,0:T(8,128)(2,1)} async-done(((bf16[2048,256]{1,0:T(8,128)(2,1)}), bf16[4096,256]{1,0:T(8,128)(2,1)}) %all-gather.9.cloned.1.call-update) | async-done | bytes 2097168 | tf_op jit(solution)/shard_map/all_gather | solution.py:23
  58.7 11.8 fusion.66
  72.4 1.8 compare_and_fusion
  74.2 178.4 %reduce-scatter.9.cloned.1.call-done = f32[1024,1536]{1,0:T(8,128)} async-done(((f32[4096,1536]{1,0:T(8,128)}), f32[1024,1536]{1,0:T(8,128)}) %reduce-scatter.9.cloned.1.call-update) | async-done | bytes 6291472 | tf_op jit(solution)/shard_map/reduce_scatter | solution.py:29
  252.6 3.2 convert_element_type.96
  255.7 1.3 fusion.63
  257.0 2.3 copy.57
  259.3 1.3 copy.56
  261.1 16.7 fusion.65
  277.8 13.0 fusion.2
  290.8 14.6 multiply_convert_fusion.2
  305.5 34.5 %all-gather.11.cloned.1.call-done = bf16[4096,512]{0,1:T(8,128)(2,1)} async-done(((bf16[1024,512]{0,1:T(8,128)(2,1)}), bf16[4096,512]{0,1:T(8,128)(2,1)}) %all-gather.11.cloned.1.call-update) | async-done | bytes 4194320 | tf_op jit(solution)/shard_map/all_gather | solution.py:39
  340.1 5.5 fusion.67
  346.3 53.9 %reduce-scatter.11.cloned.1.call-done = f32[2048,256]{1,0:T(8,128)} async-done(((f32[4096,256]{1,0:T(8,128)}), f32[2048,256]{1,0:T(8,128)}) %reduce-scatter.11.cloned.1.call-update) | async-done | bytes 2097168 | tf_op jit(solution)/shard_map/reduce_scatter | solution.py:46
  400.2 2.5 fusion.61
  402.7 11.0 all-reduce.3
  413.6 1.5 add_convert_fusion.1
  415.2 19.5 %all-gather.17.cloned.1.call-done = bf16[4096,256]{1,0:T(8,128)(2,1)} async-done(((bf16[2048,256]{1,0:T(8,128)(2,1)}), bf16[4096,256]{1,0:T(8,128)(2,1)}) %all-gather.17.cloned.1.call-update) | async-done | bytes 2097168 | tf_op jit(solution)/shard_map/all_gather | solution.py:23
  434.7 18.6 %fusion.70 = f32[4096,2048]{1,0:T(8,128)} fusion(bf16[4096,256]{1,0:T(8,128)(2,1)} %all-gather.17.cloned.1.call-done, bf16[2048,256]{1,0:T(8,128)(2,1)} %param.28), kind=kOutput, calls=%fused_computation.97 | convolution fusion | flops 4294967296 | bytes 36700160 | tf_op jit(solution)/shard_map/dot_general | solution.py:16
  453.3 16.5 all-gather.13.cloned.1.call-done
  469.8 20.5 %fusion.68 = f32[4096,2048]{1,0:T(8,128)} fusion(bf16[4096,256]{1,0:T(8,128)(2,1)} %all-gather.13.cloned.1.call-done, bf16[256,2048]{1,0:T(8,128)(2,1)S(1)} %copy-done), kind=kOutput, calls=%fused_computation.95 | convolution fusion | flops 4294967296 | bytes 36700160 | tf_op jit(solution)/shard_map/dot_general | solution.py:19
  490.4 214.3 %reduce-scatter.17.cloned.1.call-done = f32[1024,2048]{1,0:T(8,128)} async-done(((f32[4096,2048]{1,0:T(8,128)}), f32[1024,2048]{1,0:T(8,128)}) %reduce-scatter.17.cloned.1.call-update) | async-done | bytes 8388624 | tf_op jit(solution)/shard_map/reduce_scatter | solution.py:29
  704.7 234.9 %reduce-scatter.13.cloned.1.call-done = f32[1024,2048]{1,0:T(8,128)} async-done(((f32[4096,2048]{1,0:T(8,128)}), f32[1024,2048]{1,0:T(8,128)}) %reduce-scatter.13.cloned.1.call-update) | async-done | bytes 8388624 | tf_op jit(solution)/shard_map/reduce_scatter | solution.py:29
  939.7 13.0 fusion.17
  953.7 105.0 %all-gather.19.cloned.1.call-done = bf16[4096,2048]{1,0:T(8,128)(2,1)} async-done(((bf16[1024,2048]{1,0:T(8,128)(2,1)}), bf16[4096,2048]{1,0:T(8,128)(2,1)}) %all-gather.19.cloned.1.call-update) | async-done | bytes 16777232 | tf_op jit(solution)/shard_map/all_gather | solution.py:39
  1058.8 10.3 fusion.71
  1069.2 96.9 %all-gather.15.cloned.1.call-done = bf16[4096,2048]{1,0:T(8,128)(2,1)} async-done(((bf16[1024,2048]{1,0:T(8,128)(2,1)}), bf16[4096,2048]{1,0:T(8,128)(2,1)}) %all-gather.15.cloned.1.call-update) | async-done | bytes 16777232 | tf_op jit(solution)/shard_map/all_gather | solution.py:39
  1166.1 10.1 fusion.69
  1176.3 46.5 %reduce-scatter.19.cloned.1.call-done = f32[2048,256]{1,0:T(8,128)} async-done(((f32[4096,256]{1,0:T(8,128)}), f32[2048,256]{1,0:T(8,128)}) %reduce-scatter.19.cloned.1.call-update) | async-done | bytes 2097168 | tf_op jit(solution)/shard_map/reduce_scatter | solution.py:46
  1222.8 2.5 multiply_reduce_fusion.1
  1225.3 11.1 all-reduce.2
  1236.5 42.9 %reduce-scatter.15.cloned.1.call-done = f32[2048,256]{1,0:T(8,128)} async-done(((f32[4096,256]{1,0:T(8,128)}), f32[2048,256]{1,0:T(8,128)}) %reduce-scatter.15.cloned.1.call-update) | async-done | bytes 2097168 | tf_op jit(solution)/shard_map/reduce_scatter | solution.py:46
  1279.4 5.8 fusion.62
  1285.3 33.2 %all-gather.21.cloned.1.call-done = bf16[4096,256]{1,0:T(8,128)(2,1)} async-done(((bf16[2048,256]{1,0:T(8,128)(2,1)}), bf16[4096,256]{1,0:T(8,128)(2,1)}) %all-gather.21.cloned.1.call-update) | async-done | bytes 2097168 | tf_op jit(solution)/shard_map/all_gather | solution.py:23
  1318.5 6.1 fusion.72
  1324.8 71.3 %reduce-scatter.21.cloned.1.call-done = f32[1024,512]{1,0:T(8,128)} async-done(((f32[4096,512]{1,0:T(8,128)}), f32[1024,512]{1,0:T(8,128)}) %reduce-scatter.21.cloned.1.call-update) | async-done | bytes 2097168 | tf_op jit(solution)/shard_map/reduce_scatter | solution.py:29
  1396.1 1.8 select_convert_fusion
  1398.5 31.5 %fusion.43 = bf16[8,64,1024]{2,1,0:T(8,128)(2,1)} fusion(bf16[1024,8,64]{0,2,1:T(8,128)(2,1)S(1)} %bitcast.68, f32[8,1024,1024]{1,2,0:T(8,128)} %get-tuple-element.118, f32[8,1024]{1,0:T(8,128)S(1)} %log_add_fusion, bf16[1024,8,64]{0,2,1:T(8,128)(2,1)S(1)} %bitcast.63, bf16[1024,8,64]{0,2,1:T(8,128)(2,1)} %bitcast.72), kind=kOutput, calls=%fused_computation.61 | convolution fusion | flops 3280479232 | bytes 37781504 | tf_op jit(solution)/shard_map/while/body/eval_jaxpr/hqk,khd->qhd/dot_general | solution.py:127
  1430.0 33.5 %fusion.48 = bf16[8,64,1024]{2,1,0:T(8,128)(2,1)} fusion(bf16[1024,8,64]{0,2,1:T(8,128)(2,1)S(1)} %bitcast.70, f32[8,1024,1024]{1,2,0:T(8,128)} %get-tuple-element.118, f32[8,1024]{1,0:T(8,128)S(1)} %log_add_fusion, bf16[1024,8,64]{0,2,1:T(8,128)(2,1)S(1)} %bitcast.64, bf16[1024,8,64]{0,2,1:T(8,128)(2,1)} %bitcast.73), kind=kOutput, calls=%fused_computation.62 | convolution fusion | flops 3280479232 | bytes 37781504 | tf_op jit(solution)/shard_map/while/body/eval_jaxpr/hqk,qhd->khd/dot_general | solution.py:130
  1463.5 13.5 fusion.53
  1477.0 2.9 pad_maximum_fusion
  1480.2 12.8 convolution_convert_fusion
  1493.0 10.3 convolution_convert_fusion.1
  1503.3 2.0 convolution_convert_fusion.3
  1505.3 56.8 %all-gather.23.cloned.1.call-done = bf16[4096,1536]{0,1:T(8,128)(2,1)} async-done(((bf16[1024,1536]{0,1:T(8,128)(2,1)}), bf16[4096,1536]{0,1:T(8,128)(2,1)}) %all-gather.23.cloned.1.call-update) | async-done | bytes 12582928 | tf_op jit(solution)/shard_map/all_gather | solution.py:39
  1562.1 7.5 convolution_convert_fusion.2
  1570.0 10.2 fusion.73
  1580.2 1.6 copy-done.4
  1582.3 9.8 reduce_sum.166
  1592.1 12.6 all-reduce.5
  1605.3 0.6 convert_element_type.117
  1605.9 85.5 %all-reduce.9.cloned.1.call-done = (bf16[256,1536]{1,0:T(8,128)(2,1)}, bf16[512,256]{1,0:T(8,128)(2,1)}, bf16[256,2048]{1,0:T(8,128)(2,1)}, bf16[2048,256]{1,0:T(8,128)(2,1)}) async-done(((bf16[256,1536]{1,0:T(8,128)(2,1)}, bf16[512,256]{1,0:T(8,128)(2,1)}, bf16[256,2048]{1,0:T(8,128)(2,1)}, bf16[2048,256]{1,0:T(8,128)(2,1)}), (bf16[256,1536]{1,0:T(8,128)(2,1)}, bf16[512,256]{1,0:T(8,128)(2,1)}, ...) | async-done | bytes 3145744 | tf_op jit(solution)/shard_map/psum | solution.py:232
  1691.4 1.9 convert_element_type.114
  1693.3 2.9 convert_element_type.116
  1696.2 1.5 convert_element_type.119
  1697.7 1.2 fusion.64
  1698.9 48.1 %reduce-scatter.23.cloned.1.call-done = f32[2048,256]{1,0:T(8,128)} async-done(((f32[4096,256]{1,0:T(8,128)}), f32[2048,256]{1,0:T(8,128)}) %reduce-scatter.23.cloned.1.call-update) | async-done | bytes 2097168 | tf_op jit(solution)/shard_map/reduce_scatter | solution.py:46
  1747.0 2.7 fusion.41
  1749.7 10.7 all-reduce.1
  1760.5 21.0 %all-reduce = (f32[256]{0:T(256)}, f32[256]{0:T(256)}, f32[256]{0:T(256)}, f32[256]{0:T(256)}) all-reduce(f32[256]{0:T(256)S(1)} %get-tuple-element.62, f32[256]{0:T(256)S(1)} %get-tuple-element.78, f32[256]{0:T(256)S(1)} %get-tuple-element.60, f32[256]{0:T(256)S(1)} %get-tuple-element.77), channel_id=1, replica_groups=mesh['dp'=4,'row'=4,'col'=2] {'dp','col'}, use_global_device_ids=true, to_apply=%region_30.31 | all-reduce | flops 1024 | bytes 8192 | tf_op jit(solution)/shard_map/psum | solution.py:222
  1781.5 5.0 fusion.40
  (128 shorter events, 7.9 us)
Async XLA Ops:
  7.2 462.6 %copy-start = (bf16[256,2048]{1,0:T(8,128)(2,1)S(1)}, bf16[256,2048]{1,0:T(8,128)(2,1)}, u32[]{:S(2)}) copy-start(bf16[256,2048]{1,0:T(8,128)(2,1)} %param.26) | copy-start | bytes 3145732
  7.2 18.0 %copy-start.19 = (bf16[256,512]{1,0:T(8,128)(2,1)S(1)}, bf16[256,512]{1,0:T(8,128)(2,1)}, u32[]{:S(2)}) copy-start(bf16[256,512]{1,0:T(8,128)(2,1)} %param.20) | copy-start | bytes 786436
  7.2 18.0 %copy-start.20 = (bf16[256,512]{1,0:T(8,128)(2,1)S(1)}, bf16[256,512]{1,0:T(8,128)(2,1)}, u32[]{:S(2)}) copy-start(bf16[256,512]{1,0:T(8,128)(2,1)} %param.21) | copy-start | bytes 786436
  7.2 18.1 %copy-start.21 = (bf16[256,512]{1,0:T(8,128)(2,1)S(1)}, bf16[256,512]{1,0:T(8,128)(2,1)}, u32[]{:S(2)}) copy-start(bf16[256,512]{1,0:T(8,128)(2,1)} %param.22) | copy-start | bytes 786436
  7.2 51.5 %all-gather.9.cloned.1.call-start = ((), (), s32[]{:S(2)}) async-start(), calls=%async_computation.8 | async-start | bytes 3145728 | tf_op jit(solution)/shard_map/all_gather | solution.py:23
  22.0 0.6 copy-start.22
  22.0 0.6 copy-start.24
  25.1 227.4 %reduce-scatter.9.cloned.1.call-start = ((), (), s32[]{:S(2)}) async-start(), calls=%async_computation.9 | async-start | bytes 31457280 | tf_op jit(solution)/shard_map/reduce_scatter | solution.py:29
  25.3 45.1 %copy-start.12 = (bf16[256,1536]{1,0:T(8,128)(2,1)}, bf16[256,1536]{1,0:T(8,128)(2,1)S(1)}, u32[]{:S(2)}) copy-start(bf16[256,1536]{1,0:T(8,128)(2,1)S(1)} %constant_dynamic-update-slice_fusion) | copy-start | bytes 2359300
  70.4 0.7 copy-start.27
  70.4 0.7 copy-start.35
  70.4 1.9 copy-start.26
  70.5 269.6 %all-gather.11.cloned.1.call-start = ((), (), s32[]{:S(2)}) async-start(), calls=%async_computation.10 | async-start | bytes 5242880 | tf_op jit(solution)/shard_map/all_gather | solution.py:39
  72.4 180.2 %copy-start.29 = (pred[1024]{0:T(1024)(128)(4,1)}, pred[1024]{0:T(1024)(128)(4,1)S(1)}, u32[]{:S(2)}) copy-start(pred[1024]{0:T(1024)(128)(4,1)S(1)} %compare_reduce_fusion) | copy-start | bytes 3076
  261.1 29.7 %copy-start.17 = (bf16[1024,512]{0,1:T(8,128)(2,1)}, bf16[1024,512]{0,1:T(8,128)(2,1)S(1)}, u32[]{:S(2)}) copy-start(bf16[1024,512]{0,1:T(8,128)(2,1)S(1)} %copy.53) | copy-start | bytes 3145732
  290.8 49.3 %copy-start.16 = (bf16[512,256]{1,0:T(8,128)(2,1)S(1)}, bf16[512,256]{1,0:T(8,128)(2,1)}, u32[]{:S(2)}) copy-start(bf16[512,256]{1,0:T(8,128)(2,1)} %param.23) | copy-start | bytes 786436
  305.5 94.7 %reduce-scatter.11.cloned.1.call-start = ((), (), s32[]{:S(2)}) async-start(), calls=%async_computation.11 | async-start | bytes 6291456 | tf_op jit(solution)/shard_map/reduce_scatter | solution.py:46
  345.6 68.0 %copy-start.28 = (f32[256]{0:T(256)S(1)}, f32[256]{0:T(256)}, u32[]{:S(2)}) copy-start(f32[256]{0:T(256)} %param.24) | copy-start | bytes 3076
  345.6 68.0 %copy-start.33 = (f32[256]{0:T(256)S(1)}, f32[256]{0:T(256)}, u32[]{:S(2)}) copy-start(f32[256]{0:T(256)} %param.25) | copy-start | bytes 3076
  345.7 89.0 %all-gather.17.cloned.1.call-start = ((), (), s32[]{:S(2)}) async-start(), calls=%async_computation.16 | async-start | bytes 3145728 | tf_op jit(solution)/shard_map/all_gather | solution.py:23
  346.2 123.5 %all-gather.13.cloned.1.call-start = ((), (), s32[]{:S(2)}) async-start(), calls=%async_computation.12 | async-start | bytes 3145728 | tf_op jit(solution)/shard_map/all_gather | solution.py:23
  415.2 289.6 %reduce-scatter.17.cloned.1.call-start = ((), (), s32[]{:S(2)}) async-start(), calls=%async_computation.17 | async-start | bytes 41943040 | tf_op jit(solution)/shard_map/reduce_scatter | solution.py:29
  453.3 486.4 %reduce-scatter.13.cloned.1.call-start = ((), (), s32[]{:S(2)}) async-start(), calls=%async_computation.13 | async-start | bytes 41943040 | tf_op jit(solution)/shard_map/reduce_scatter | solution.py:29
  490.3 449.4 %copy-start.32 = (f32[2048]{0:T(1024)S(1)}, f32[2048]{0:T(1024)}, u32[]{:S(2)}) copy-start(f32[2048]{0:T(1024)} %param.27) | copy-start | bytes 24580
  490.3 568.4 %all-gather.19.cloned.1.call-start = ((), (), s32[]{:S(2)}) async-start(), calls=%async_computation.18 | async-start | bytes 20971520 | tf_op jit(solution)/shard_map/all_gather | solution.py:39
  952.7 213.4 %all-gather.15.cloned.1.call-start = ((), (), s32[]{:S(2)}) async-start(), calls=%async_computation.14 | async-start | bytes 20971520 | tf_op jit(solution)/shard_map/all_gather | solution.py:39
  953.3 269.5 %reduce-scatter.19.cloned.1.call-start = ((), (), s32[]{:S(2)}) async-start(), calls=%async_computation.19 | async-start | bytes 6291456 | tf_op jit(solution)/shard_map/reduce_scatter | solution.py:46
  1069.1 97.0 %copy-start.14 = (bf16[2048,256]{1,0:T(8,128)(2,1)S(1)}, bf16[2048,256]{1,0:T(8,128)(2,1)}, u32[]{:S(2)}) copy-start(bf16[2048,256]{1,0:T(8,128)(2,1)} %param.28) | copy-start | bytes 3145732
  1069.1 210.2 %reduce-scatter.15.cloned.1.call-start = ((), (), s32[]{:S(2)}) async-start(), calls=%async_computation.15 | async-start | bytes 6291456 | tf_op jit(solution)/shard_map/reduce_scatter | solution.py:46
  1176.2 103.2 %copy-start.6 = (bf16[2048,256]{1,0:T(8,128)(2,1)S(1)}, bf16[2048,256]{1,0:T(8,128)(2,1)}, u32[]{:S(2)}) copy-start(bf16[2048,256]{1,0:T(8,128)(2,1)} %param.33) | copy-start | bytes 3145732
  1176.2 103.2 %copy-start.34 = (f32[256]{0:T(256)S(1)}, f32[256]{0:T(256)}, u32[]{:S(2)}) copy-start(f32[256]{0:T(256)} %param.29) | copy-start | bytes 3076
  1176.2 142.3 %all-gather.21.cloned.1.call-start = ((), (), s32[]{:S(2)}) async-start(), calls=%async_computation.20 | async-start | bytes 3145728 | tf_op jit(solution)/shard_map/all_gather | solution.py:23
  1285.2 110.9 %reduce-scatter.21.cloned.1.call-start = ((), (), s32[]{:S(2)}) async-start(), calls=%async_computation.21 | async-start | bytes 10485760 | tf_op jit(solution)/shard_map/reduce_scatter | solution.py:29
  1324.5 71.6 %copy-start.30 = (pred[1024]{0:T(1024)(128)(4,1)S(1)}, pred[1024]{0:T(1024)(128)(4,1)}, u32[]{:S(2)}) copy-start(pred[1024]{0:T(1024)(128)(4,1)} %copy-done.29) | copy-start | bytes 3076
  1324.6 73.9 %copy-start.7 = (bf16[1024,512]{0,1:T(8,128)(2,1)S(1)}, bf16[1024,512]{0,1:T(8,128)(2,1)}, u32[]{:S(2)}) copy-start(bf16[1024,512]{0,1:T(8,128)(2,1)} %copy.57) | copy-start | bytes 3145732
  1324.6 237.5 %all-gather.23.cloned.1.call-start = ((), (), s32[]{:S(2)}) async-start(), calls=%async_computation.22 | async-start | bytes 15728640 | tf_op jit(solution)/shard_map/all_gather | solution.py:39
  1398.5 31.5 %copy-start.8 = (bf16[1024,512]{0,1:T(8,128)(2,1)S(1)}, bf16[1024,512]{0,1:T(8,128)(2,1)}, u32[]{:S(2)}) copy-start(bf16[1024,512]{0,1:T(8,128)(2,1)} %copy.56) | copy-start | bytes 3145732
  1463.5 13.5 copy-start.18
  1479.9 13.1 copy-start.3
  1479.9 211.5 %all-reduce.9.cloned.1.call-start = ((), (), s32[]{:S(2)}) async-start(), calls=%async_computation.24 | async-start | bytes 6291456 | tf_op jit(solution)/shard_map/psum | solution.py:232
  1493.0 10.3 copy-start.5
  1493.0 10.3 copy-start.10
  1503.3 58.8 %copy-start.9 = (bf16[4096,256]{1,0:T(8,128)(2,1)S(1)}, bf16[4096,256]{1,0:T(8,128)(2,1)}, u32[]{:S(2)}) copy-start(bf16[4096,256]{1,0:T(8,128)(2,1)} %all-gather.9.cloned.1.call-done) | copy-start | bytes 6291460
  1505.3 64.6 %copy-start.13 = (bf16[256,1536]{1,0:T(8,128)(2,1)S(1)}, bf16[256,1536]{1,0:T(8,128)(2,1)}, u32[]{:S(2)}) copy-start(bf16[256,1536]{1,0:T(8,128)(2,1)} %copy-done.12) | copy-start | bytes 2359300
  1569.6 177.3 %reduce-scatter.23.cloned.1.call-start = ((), (), s32[]{:S(2)}) async-start(), calls=%async_computation.23 | async-start | bytes 6291456 | tf_op jit(solution)/shard_map/reduce_scatter | solution.py:46
  1580.2 1.6 copy-start.4
  1691.4 4.8 copy-start.15
  1691.4 6.3 copy-start.11
  1693.3 53.7 %copy-start.2 = (bf16[2048,256]{1,0:T(8,128)(2,1)S(1)}, bf16[2048,256]{1,0:T(8,128)(2,1)}, u32[]{:S(2)}) copy-start(bf16[2048,256]{1,0:T(8,128)(2,1)} %param.17) | copy-start | bytes 3145732
  1693.3 53.7 %copy-start.23 = (f32[2048]{0:T(1024)S(1)}, f32[2048]{0:T(1024)}, u32[]{:S(2)}) copy-start(f32[2048]{0:T(1024)} %copy-done.22) | copy-start | bytes 24580
  1693.3 53.7 %copy-start.25 = (f32[2048]{0:T(1024)S(1)}, f32[2048]{0:T(1024)}, u32[]{:S(2)}) copy-start(f32[2048]{0:T(1024)} %copy-done.24) | copy-start | bytes 24580
  1693.3 53.7 %copy-start.31 = (f32[256]{0:T(256)S(1)}, f32[256]{0:T(256)}, u32[]{:S(2)}) copy-start(f32[256]{0:T(256)} %param.18) | copy-start | bytes 3076
  1747.0 39.5 %copy-start.1 = (bf16[256,2048]{1,0:T(8,128)(2,1)S(1)}, bf16[256,2048]{1,0:T(8,128)(2,1)}, u32[]{:S(2)}) copy-start(bf16[256,2048]{1,0:T(8,128)(2,1)} %param.26) | copy-start | bytes 3145732
Sparse Core Ops, SparseCore 0:
  25.3 33.3 all-gather.8
  70.6 181.9 reduce-scatter.8
  305.6 34.4 all-gather.10
  345.8 54.3 reduce-scatter.10
  401.6 33.0 all-gather.16
  436.7 33.0 all-gather.12
  472.4 232.3 reduce-scatter.16
  707.3 232.3 reduce-scatter.12
  952.8 105.9 all-gather.18
  1060.2 105.8 all-gather.14
  1168.4 54.3 reduce-scatter.18
  1225.0 54.3 reduce-scatter.14
  1285.4 33.0 all-gather.20
  1324.7 71.3 reduce-scatter.20
  1480.0 82.0 all-gather.22
  1569.8 121.6 all-reduce.8
  1693.6 53.3 reduce-scatter.22
where the time goes:
time: 1800 us; the launch traced here: 1790 us
  waiting for transfers between devices  1370 us (76%)
  matrix products  235 us (13%)
  blocking collectives  79.2 us (4%)
  other arithmetic  78.4 us (4%)
    reduce_scatter x4, waiting for transfers between devices, to_columns(): lax.psum_scatter(term_rows(jnp.int32(0), lax.axis_size('row') * row_count...  699 us
    all_gather x4, waiting for transfers between devices, to_rows(): gathered = lax.all_gather(moving, 'row', axis=0, tiled=True)  293 us
    reduce_scatter x4, waiting for transfers between devices, to_rows(): lax.psum_scatter(term_rows(jnp.int32(0), lax.axis_size('col') * row_count...  191 us
    all_gather x4, waiting for transfers between devices, to_columns(): gathered = lax.all_gather(moving, 'col', axis=0, tiled=True)  103 us
    psum x1, waiting for transfers between devices, body(): lax.psum(grad_stacked.astype(jnp.bfloat16), 'dp').astype(jnp.float32)  85.5 us
    dot_general x4, matrix products, product(): return jnp.dot(picked, weight, preferred_element_type=jnp.float32)  47.9 us
    psum x4, blocking collectives, norm_sums(): return lax.psum((first_sum, second_sum), 'row')  45.5 us
    dot_general x4, matrix products, product(): lax.dot_general(picked, weight, (((1,), (1,)), ((), ())), preferred_eleme...  45.2 us
  transfers between devices with their start and end apart: 17, of which 17 were waited for; matrix products, arithmetic and copies ran while one was open for 7% of the time, Pallas kernels for 0%

commit v1 on v0

--- a/solution.py
+++ b/solution.py
@@ -11,6 +11,27 @@
 EPS = 1e-05
 
 
+def collect(shard, axis, dim):
+    devices, position, width = (lax.axis_size(axis), lax.axis_index(axis), shard.shape[dim])
+    forward = [(i, (i + 1) % devices) for i in range(devices)]
+    downward = [(i, (i - 1) % devices) for i in range(devices)]
+    out = jnp.zeros((*shard.shape[:dim], devices * width, *shard.shape[dim + 1 :]), shard.dtype)
+    out = lax.dynamic_update_slice_in_dim(out, shard, position * width, axis=dim)
+    from_left = from_right = shard
+    half = devices // 2
+    for step in range(1, half + 1):
+        from_left = lax.ppermute(from_left, axis, forward)
+        out = lax.dynamic_update_slice_in_dim(
+            out, from_left, (position - step) % devices * width, axis=dim
+        )
+        if step < devices - half:
+            from_right = lax.ppermute(from_right, axis, downward)
+            out = lax.dynamic_update_slice_in_dim(
+                out, from_right, (position + step) % devices * width, axis=dim
+            )
+    return out
+
+
 def product(picked, weight, flipped):
     if flipped:
         return lax.dot_general(
@@ -36,7 +57,7 @@
 
 
 def to_rows(moving, weight, flipped):
-    gathered = lax.all_gather(moving, "row", axis=0, tiled=True)
+    gathered = collect(moving, "row", 0)
     row_count = gathered.shape[0] // lax.axis_size("col")
 
     def term_rows(first_row, how_many):

time: 1800 us -> 1850 us (1.028)
  local copies, waits for them, and re-layouts: 10.8 us -> 64.4 us
    ppermute x0 -> x12, waiting for transfers between devices: none -> 350 us  [the longest x8 326 us: collect(): from_left = lax.ppermute(from_left, axis, forward)]
    all_gather x4 -> x0, waiting for transfers between devices: 293 us -> none  [to_rows(): gathered = lax.all_gather(moving, 'row', axis=0, tiled=True)]
    reduce_scatter x4, waiting for transfers between devices: 191 us -> 142 us  [to_rows(): lax.psum_scatter(term_rows(jnp.int32(0), lax.axis_size('col') * row_count...]
    dynamic_update_slice x0 -> x13, local copies, waits for them, and re-layouts: none -> 30.2 us  [the longest x8 19.6 us: collect(): lax.dynamic_update_slice_in_dim(out, from_left, (position - step) % devic...]
  transfers between devices with their start and end apart: 17 -> 25, of which waited for: 17 -> 21; matrix products, arithmetic and copies ran while one was open for 7% -> 8% of each run, Pallas kernels for 0% -> 0%
where the time goes in v1:
time: 1850 us
  waiting for transfers between devices  1380 us (75%)
  matrix products  222 us (12%)
  other arithmetic  83.3 us (5%)
  blocking collectives  78.4 us (4%)
  local copies, waits for them, and re-layouts  64.4 us (3%)
    reduce_scatter x4, waiting for transfers between devices, to_columns(): lax.psum_scatter(term_rows(jnp.int32(0), lax.axis_size('row') * row_count...  698 us
    ppermute x8, waiting for transfers between devices, collect(): from_left = lax.ppermute(from_left, axis, forward)  326 us
    reduce_scatter x4, waiting for transfers between devices, to_rows(): lax.psum_scatter(term_rows(jnp.int32(0), lax.axis_size('col') * row_count...  142 us
    all_gather x4, waiting for transfers between devices, to_columns(): gathered = lax.all_gather(moving, 'col', axis=0, tiled=True)  99.9 us
    psum x1, waiting for transfers between devices, body(): lax.psum(grad_stacked.astype(jnp.bfloat16), 'dp').astype(jnp.float32)  86.8 us
    dot_general x4, matrix products, product(): return jnp.dot(picked, weight, preferred_element_type=jnp.float32)  45.9 us
    psum x4, blocking collectives, norm_sums(): return lax.psum((first_sum, second_sum), 'row')  44.8 us
    dot_general x4, matrix products, product(): lax.dot_general(picked, weight, (((1,), (1,)), ((), ())), preferred_eleme...  41 us
  transfers between devices with their start and end apart: 25, of which 21 were waited for; matrix products, arithmetic and copies ran while one was open for 8% of the time, Pallas kernels for 0%

profile of v1, /device:TPU:0, one launch (start us, length us, event | category | flops | bytes accessed | tf_op | source)
XLA Modules:
  0.0 1848.0 jit_solution(4975989300616727920)
XLA Ops:
  9.2 12.7 all-reduce.4
  28.1 30.6 %all-gather.5.cloned.1.call-done = bf16[4096,256]{1,0:T(8,128)(2,1)} async-done(((bf16[2048,256]{1,0:T(8,128)(2,1)}), bf16[4096,256]{1,0:T(8,128)(2,1)}) %all-gather.5.cloned.1.call-update) | async-done | bytes 2097168 | tf_op jit(solution)/shard_map/all_gather | solution.py:44
  58.6 11.8 fusion.67
  74.1 178.4 %reduce-scatter.9.cloned.1.call-done = f32[1024,1536]{1,0:T(8,128)} async-done(((f32[4096,1536]{1,0:T(8,128)}), f32[1024,1536]{1,0:T(8,128)}) %reduce-scatter.9.cloned.1.call-update) | async-done | bytes 6291472 | tf_op jit(solution)/shard_map/reduce_scatter | solution.py:50
  252.5 3.2 convert_element_type.96
  261.0 16.3 fusion.66
  277.4 13.1 fusion.2
  290.5 13.6 multiply_convert_fusion.2
  306.0 23.1 %collective-permute-done = bf16[1024,512]{0,1:T(8,128)(2,1)S(1)} collective-permute-done((bf16[1024,512]{0,1:T(8,128)(2,1)S(1)}, bf16[1024,512]{0,1:T(8,128)(2,1)S(1)}, u32[]{:S(2)}, u32[]{:S(2)}) %collective-permute-start) | collective-permute-done | bytes 1048608 | tf_op jit(solution)/shard_map/ppermute | solution.py:23
  331.5 12.1 collective-permute-done.2
  346.9 3.4 fusion.68
  350.9 53.6 %reduce-scatter.11.cloned.1.call-done = f32[2048,256]{1,0:T(8,128)} async-done(((f32[4096,256]{1,0:T(8,128)}), f32[2048,256]{1,0:T(8,128)}) %reduce-scatter.11.cloned.1.call-update) | async-done | bytes 2097168 | tf_op jit(solution)/shard_map/reduce_scatter | solution.py:67
  407.0 10.8 all-reduce.3
  419.4 19.7 %all-gather.9.cloned.1.call-done = bf16[4096,256]{1,0:T(8,128)(2,1)} async-done(((bf16[2048,256]{1,0:T(8,128)(2,1)}), bf16[4096,256]{1,0:T(8,128)(2,1)}) %all-gather.9.cloned.1.call-update) | async-done | bytes 2097168 | tf_op jit(solution)/shard_map/all_gather | solution.py:44
  439.1 18.6 %fusion.71 = f32[4096,2048]{1,0:T(8,128)} fusion(bf16[4096,256]{1,0:T(8,128)(2,1)} %all-gather.9.cloned.1.call-done, bf16[2048,256]{1,0:T(8,128)(2,1)} %param.28), kind=kOutput, calls=%fused_computation.113 | convolution fusion | flops 4294967296 | bytes 36700160 | tf_op jit(solution)/shard_map/dot_general | solution.py:37
  457.7 16.5 all-gather.7.cloned.1.call-done
  474.2 20.7 %fusion.69 = f32[4096,2048]{1,0:T(8,128)} fusion(bf16[4096,256]{1,0:T(8,128)(2,1)} %all-gather.7.cloned.1.call-done, bf16[256,2048]{1,0:T(8,128)(2,1)S(1)} %copy-done), kind=kOutput, calls=%fused_computation.111 | convolution fusion | flops 4294967296 | bytes 36700160 | tf_op jit(solution)/shard_map/dot_general | solution.py:40
  495.4 213.6 %reduce-scatter.17.cloned.1.call-done = f32[1024,2048]{1,0:T(8,128)} async-done(((f32[4096,2048]{1,0:T(8,128)}), f32[1024,2048]{1,0:T(8,128)}) %reduce-scatter.17.cloned.1.call-update) | async-done | bytes 8388624 | tf_op jit(solution)/shard_map/reduce_scatter | solution.py:50
  709.0 234.9 %reduce-scatter.13.cloned.1.call-done = f32[1024,2048]{1,0:T(8,128)} async-done(((f32[4096,2048]{1,0:T(8,128)}), f32[1024,2048]{1,0:T(8,128)}) %reduce-scatter.13.cloned.1.call-update) | async-done | bytes 8388624 | tf_op jit(solution)/shard_map/reduce_scatter | solution.py:50
  946.0 9.5 constant_dynamic-update-slice_fusion.10
  957.3 90.5 %collective-permute-done.6 = bf16[1024,2048]{1,0:T(8,128)(2,1)S(1)} collective-permute-done((bf16[1024,2048]{1,0:T(8,128)(2,1)S(1)}, bf16[1024,2048]{1,0:T(8,128)(2,1)S(1)}, u32[]{:S(2)}, u32[]{:S(2)}) %collective-permute-start.6) | collective-permute-done | bytes 4194336 | tf_op jit(solution)/shard_map/ppermute | solution.py:23
  1047.8 6.0 broadcast.127.clone.1
  1053.8 7.2 constant_dynamic-update-slice_fusion.14
  1061.6 2.8 constant_dynamic-update-slice_fusion.8
  1064.4 31.4 %collective-permute-done.8 = bf16[1024,2048]{1,0:T(8,128)(2,1)} collective-permute-done((bf16[1024,2048]{1,0:T(8,128)(2,1)S(1)}, bf16[1024,2048]{1,0:T(8,128)(2,1)}, u32[]{:S(2)}, u32[]{:S(2)}) %collective-permute-start.8) | collective-permute-done | bytes 4194336 | tf_op jit(solution)/shard_map/ppermute | solution.py:23
  1095.8 2.8 constant_dynamic-update-slice_fusion.7
  1098.7 5.7 copy-done.2
  1104.4 6.2 fusion.72
  1110.7 59.3 %collective-permute-done.3 = bf16[1024,2048]{1,0:T(8,128)(2,1)} collective-permute-done((bf16[1024,2048]{1,0:T(8,128)(2,1)}, bf16[1024,2048]{1,0:T(8,128)(2,1)}, u32[]{:S(2)}, u32[]{:S(2)}) %collective-permute-start.3) | collective-permute-done | bytes 4194336 | tf_op jit(solution)/shard_map/ppermute | solution.py:23
  1170.0 4.7 constant_dynamic-update-slice_fusion.13
  1174.7 24.0 %collective-permute-done.4 = bf16[1024,2048]{1,0:T(8,128)(2,1)S(1)} collective-permute-done((bf16[1024,2048]{1,0:T(8,128)(2,1)}, bf16[1024,2048]{1,0:T(8,128)(2,1)S(1)}, u32[]{:S(2)}, u32[]{:S(2)}) %collective-permute-start.4) | collective-permute-done | bytes 4194336 | tf_op jit(solution)/shard_map/ppermute | solution.py:28
  1200.9 29.6 %collective-permute-done.5 = bf16[1024,2048]{1,0:T(8,128)(2,1)S(1)} collective-permute-done((bf16[1024,2048]{1,0:T(8,128)(2,1)}, bf16[1024,2048]{1,0:T(8,128)(2,1)S(1)}, u32[]{:S(2)}, u32[]{:S(2)}) %collective-permute-start.5) | collective-permute-done | bytes 4194336 | tf_op jit(solution)/shard_map/ppermute | solution.py:23
  1232.8 10.1 fusion.70
  1243.0 2.6 multiply_reduce_fusion.1
  1245.6 10.5 all-reduce.2
  1256.1 41.1 %reduce-scatter.15.cloned.1.call-done = f32[2048,256]{1,0:T(8,128)} async-done(((f32[4096,256]{1,0:T(8,128)}), f32[2048,256]{1,0:T(8,128)}) %reduce-scatter.15.cloned.1.call-update) | async-done | bytes 2097168 | tf_op jit(solution)/shard_map/reduce_scatter | solution.py:67
  1297.2 5.8 fusion.62
  1303.1 33.2 %all-gather.11.cloned.1.call-done = bf16[4096,256]{1,0:T(8,128)(2,1)} async-done(((bf16[2048,256]{1,0:T(8,128)(2,1)}), bf16[4096,256]{1,0:T(8,128)(2,1)}) %all-gather.11.cloned.1.call-update) | async-done | bytes 2097168 | tf_op jit(solution)/shard_map/all_gather | solution.py:44
  1336.4 6.1 fusion.73
  1342.5 71.5 %reduce-scatter.21.cloned.1.call-done = f32[1024,512]{1,0:T(8,128)} async-done(((f32[4096,512]{1,0:T(8,128)}), f32[1024,512]{1,0:T(8,128)}) %reduce-scatter.21.cloned.1.call-update) | async-done | bytes 2097168 | tf_op jit(solution)/shard_map/reduce_scatter | solution.py:50
  1416.6 13.5 fusion.53
  1430.1 33.7 %fusion.48 = bf16[8,64,1024]{2,1,0:T(8,128)(2,1)} fusion(bf16[1024,8,64]{0,2,1:T(8,128)(2,1)S(1)} %bitcast.70, f32[8,1024,1024]{1,2,0:T(8,128)} %get-tuple-element.122, f32[8,1024]{1,0:T(8,128)S(1)} %log_add_fusion, bf16[1024,8,64]{0,2,1:T(8,128)(2,1)S(1)} %bitcast.67, bf16[1024,8,64]{0,2,1:T(8,128)(2,1)} %bitcast.78), kind=kOutput, calls=%fused_computation.62 | convolution fusion | flops 3280479232 | bytes 37781504 | tf_op jit(solution)/shard_map/while/body/eval_jaxpr/hqk,qhd->khd/dot_general | solution.py:151
  1463.8 33.2 %fusion.43 = bf16[8,64,1024]{2,1,0:T(8,128)(2,1)} fusion(bf16[1024,8,64]{0,2,1:T(8,128)(2,1)} %bitcast.72, f32[8,1024,1024]{1,2,0:T(8,128)} %get-tuple-element.122, f32[8,1024]{1,0:T(8,128)S(1)} %log_add_fusion, bf16[1024,8,64]{0,2,1:T(8,128)(2,1)S(1)} %bitcast.68, bf16[1024,8,64]{0,2,1:T(8,128)(2,1)} %bitcast.79), kind=kOutput, calls=%fused_computation.61 | convolution fusion | flops 3280479232 | bytes 37781504 | tf_op jit(solution)/shard_map/while/body/eval_jaxpr/hqk,khd->qhd/dot_general | solution.py:148
  1497.0 6.1 broadcast_in_dim.59
  1503.1 3.0 pad_maximum_fusion
  1508.1 68.0 %collective-permute-done.9 = bf16[1024,1536]{0,1:T(8,128)(2,1)} collective-permute-done((bf16[1024,1536]{0,1:T(8,128)(2,1)}, bf16[1024,1536]{0,1:T(8,128)(2,1)}, u32[]{:S(2)}, u32[]{:S(2)}) %collective-permute-start.9) | collective-permute-done | bytes 3145760 | tf_op jit(solution)/shard_map/ppermute | solution.py:23
  1576.1 9.4 convolution_convert_fusion
  1585.6 5.5 convolution_convert_fusion.1
  1593.0 3.9 constant_dynamic-update-slice_fusion.5
  1596.9 4.0 constant_dynamic-update-slice_fusion.4
  1600.9 12.2 collective-permute-done.11
  1613.1 3.9 constant_dynamic-update-slice_fusion.3
  1617.0 7.5 convolution_convert_fusion.2
  1624.9 10.2 fusion.74
  1635.7 9.8 reduce_sum.166
  1645.5 12.6 all-reduce.5
  1659.3 86.8 %all-reduce.9.cloned.1.call-done = (bf16[256,1536]{1,0:T(8,128)(2,1)}, bf16[512,256]{1,0:T(8,128)(2,1)}, bf16[256,2048]{1,0:T(8,128)(2,1)}, bf16[2048,256]{1,0:T(8,128)(2,1)}) async-done(((bf16[256,1536]{1,0:T(8,128)(2,1)}, bf16[512,256]{1,0:T(8,128)(2,1)}, bf16[256,2048]{1,0:T(8,128)(2,1)}, bf16[2048,256]{1,0:T(8,128)(2,1)}), (bf16[256,1536]{1,0:T(8,128)(2,1)}, bf16[512,256]{1,0:T(8,128)(2,1)}, ...) | async-done | bytes 3145744 | tf_op jit(solution)/shard_map/psum | solution.py:253
  1747.9 2.8 convert_element_type.116
  1750.7 2.7 convert_element_type.119
  1754.6 47.2 %reduce-scatter.23.cloned.1.call-done = f32[2048,256]{1,0:T(8,128)} async-done(((f32[4096,256]{1,0:T(8,128)}), f32[2048,256]{1,0:T(8,128)}) %reduce-scatter.23.cloned.1.call-update) | async-done | bytes 2097168 | tf_op jit(solution)/shard_map/reduce_scatter | solution.py:67
  1801.8 2.6 fusion.41
  1804.4 10.7 all-reduce.1
  1815.2 21.0 %all-reduce = (f32[256]{0:T(256)}, f32[256]{0:T(256)}, f32[256]{0:T(256)}, f32[256]{0:T(256)}) all-reduce(f32[256]{0:T(256)S(1)} %get-tuple-element.62, f32[256]{0:T(256)S(1)} %get-tuple-element.78, f32[256]{0:T(256)S(1)} %get-tuple-element.60, f32[256]{0:T(256)S(1)} %get-tuple-element.77), channel_id=1, replica_groups=mesh['dp'=4,'row'=4,'col'=2] {'dp','col'}, use_global_device_ids=true, to_apply=%region_30.31 | all-reduce | flops 1024 | bytes 8192 | tf_op jit(solution)/shard_map/psum | solution.py:243
  1836.2 5.0 fusion.40
  (165 shorter events, 50.6 us)
Async XLA Ops:
  7.2 467.0 %copy-start = (bf16[256,2048]{1,0:T(8,128)(2,1)S(1)}, bf16[256,2048]{1,0:T(8,128)(2,1)}, u32[]{:S(2)}) copy-start(bf16[256,2048]{1,0:T(8,128)(2,1)} %param.26) | copy-start | bytes 3145732
  7.2 51.4 %all-gather.5.cloned.1.call-start = ((), (), s32[]{:S(2)}) async-start(), calls=%async_computation.8 | async-start | bytes 3145728 | tf_op jit(solution)/shard_map/all_gather | solution.py:44
  21.9 0.6 copy-start.21
  21.9 0.6 copy-start.23
  25.1 227.5 %reduce-scatter.9.cloned.1.call-start = ((), (), s32[]{:S(2)}) async-start(), calls=%async_computation.9 | async-start | bytes 31457280 | tf_op jit(solution)/shard_map/reduce_scatter | solution.py:50
  28.0 42.4 %copy-start.14 = (bf16[256,1536]{1,0:T(8,128)(2,1)}, bf16[256,1536]{1,0:T(8,128)(2,1)S(1)}, u32[]{:S(2)}) copy-start(bf16[256,1536]{1,0:T(8,128)(2,1)S(1)} %constant_dynamic-update-slice_fusion) | copy-start | bytes 2359300
  70.4 0.7 copy-start.27
  70.4 0.7 copy-start.34
  70.4 1.9 copy-start.25
  70.4 334.1 %reduce-scatter.11.cloned.1.call-start = ((), (), s32[]{:S(2)}) async-start(), calls=%async_computation.10 | async-start | bytes 6291456 | tf_op jit(solution)/shard_map/reduce_scatter | solution.py:67
  72.3 180.2 %copy-start.29 = (pred[1024]{0:T(1024)(128)(4,1)}, pred[1024]{0:T(1024)(128)(4,1)S(1)}, u32[]{:S(2)}) copy-start(pred[1024]{0:T(1024)(128)(4,1)S(1)} %compare_reduce_fusion) | copy-start | bytes 3076
  261.0 16.4 copy-start.10
  277.4 13.1 copy-start.20
  304.2 24.9 %collective-permute-start = (bf16[1024,512]{0,1:T(8,128)(2,1)S(1)}, bf16[1024,512]{0,1:T(8,128)(2,1)S(1)}, u32[]{:S(2)}, u32[]{:S(2)}) collective-permute-start(bf16[1024,512]{0,1:T(8,128)(2,1)S(1)} %bitcast.75), channel_id=1, source_target_pairs={{0,2},{2,4},{4,6},{6,0},{1,3},{3,5},{5,7},{7,1},{8,10},{10,12},{12... | collective-permute-start | bytes 3145736 | tf_op jit(solution)/shard_map/ppermute | solution.py:23
  304.3 25.9 %collective-permute-start.1 = (bf16[1024,512]{0,1:T(8,128)(2,1)S(1)}, bf16[1024,512]{0,1:T(8,128)(2,1)}, u32[]{:S(2)}, u32[]{:S(2)}) collective-permute-start(bf16[1024,512]{0,1:T(8,128)(2,1)S(1)} %bitcast.76), channel_id=1, source_target_pairs={{0,6},{2,0},{4,2},{6,4},{1,7},{3,1},{5,3},{7,5},{8,14},{10,8},{12,... | collective-permute-start | bytes 3145736 | tf_op jit(solution)/shard_map/ppermute | solution.py:28
  329.1 14.5 collective-permute-start.2
  329.3 17.6 copy-start.19
  344.9 2.0 copy-start.4
  350.3 67.5 %copy-start.28 = (f32[256]{0:T(256)S(1)}, f32[256]{0:T(256)}, u32[]{:S(2)}) copy-start(f32[256]{0:T(256)} %param.24) | copy-start | bytes 3076
  350.3 67.5 %copy-start.32 = (f32[256]{0:T(256)S(1)}, f32[256]{0:T(256)}, u32[]{:S(2)}) copy-start(f32[256]{0:T(256)} %param.25) | copy-start | bytes 3076
  350.3 88.8 %all-gather.9.cloned.1.call-start = ((), (), s32[]{:S(2)}) async-start(), calls=%async_computation.14 | async-start | bytes 3145728 | tf_op jit(solution)/shard_map/all_gather | solution.py:44
  350.9 123.3 %all-gather.7.cloned.1.call-start = ((), (), s32[]{:S(2)}) async-start(), calls=%async_computation.11 | async-start | bytes 3145728 | tf_op jit(solution)/shard_map/all_gather | solution.py:44
  419.3 289.6 %reduce-scatter.17.cloned.1.call-start = ((), (), s32[]{:S(2)}) async-start(), calls=%async_computation.15 | async-start | bytes 41943040 | tf_op jit(solution)/shard_map/reduce_scatter | solution.py:50
  457.7 486.3 %reduce-scatter.13.cloned.1.call-start = ((), (), s32[]{:S(2)}) async-start(), calls=%async_computation.12 | async-start | bytes 41943040 | tf_op jit(solution)/shard_map/reduce_scatter | solution.py:50
  494.9 451.1 %copy-start.26 = (f32[2048]{0:T(1024)S(1)}, f32[2048]{0:T(1024)}, u32[]{:S(2)}) copy-start(f32[2048]{0:T(1024)} %param.27) | copy-start | bytes 24580
  494.9 748.0 %reduce-scatter.19.cloned.1.call-start = ((), (), s32[]{:S(2)}) async-start(), calls=%async_computation.16 | async-start | bytes 6291456 | tf_op jit(solution)/shard_map/reduce_scatter | solution.py:67
  955.5 92.3 %collective-permute-start.6 = (bf16[1024,2048]{1,0:T(8,128)(2,1)S(1)}, bf16[1024,2048]{1,0:T(8,128)(2,1)S(1)}, u32[]{:S(2)}, u32[]{:S(2)}) collective-permute-start(bf16[1024,2048]{1,0:T(8,128)(2,1)S(1)} %get-tuple-element.104), channel_id=1, source_target_pairs={{0,2},{2,4},{4,6},{6,0},{1,3},{3,5},{5,7},{7,1},{8,10},{10,12},{12... | collective-permute-start | bytes 12582920 | tf_op jit(solution)/shard_map/ppermute | solution.py:23
  955.6 106.0 %collective-permute-start.7 = (bf16[1024,2048]{1,0:T(8,128)(2,1)S(1)}, bf16[1024,2048]{1,0:T(8,128)(2,1)}, u32[]{:S(2)}, u32[]{:S(2)}) collective-permute-start(bf16[1024,2048]{1,0:T(8,128)(2,1)S(1)} %get-tuple-element.104), channel_id=1, source_target_pairs={{0,6},{2,0},{4,2},{6,4},{1,7},{3,1},{5,3},{7,5},{8,14},{10,8},{12,... | collective-permute-start | bytes 12582920 | tf_op jit(solution)/shard_map/ppermute | solution.py:28
  1047.8 48.0 %collective-permute-start.8 = (bf16[1024,2048]{1,0:T(8,128)(2,1)S(1)}, bf16[1024,2048]{1,0:T(8,128)(2,1)}, u32[]{:S(2)}, u32[]{:S(2)}) collective-permute-start(bf16[1024,2048]{1,0:T(8,128)(2,1)S(1)} %collective-permute-done.6), channel_id=1, source_target_pairs={{0,2},{2,4},{4,6},{6,0},{1,3},{3,5},{5,7},{7,1},{8,10},{10,12},{12... | collective-permute-start | bytes 12582920 | tf_op jit(solution)/shard_map/ppermute | solution.py:23
  1061.0 109.0 %collective-permute-start.3 = (bf16[1024,2048]{1,0:T(8,128)(2,1)}, bf16[1024,2048]{1,0:T(8,128)(2,1)}, u32[]{:S(2)}, u32[]{:S(2)}) collective-permute-start(bf16[1024,2048]{1,0:T(8,128)(2,1)} %get-tuple-element.106), channel_id=1, source_target_pairs={{0,2},{2,4},{4,6},{6,0},{1,3},{3,5},{5,7},{7,1},{8,10},{10,12},{12... | collective-permute-start | bytes 12582920 | tf_op jit(solution)/shard_map/ppermute | solution.py:23
  1098.7 5.7 copy-start.2
  1110.6 186.7 %reduce-scatter.15.cloned.1.call-start = ((), (), s32[]{:S(2)}) async-start(), calls=%async_computation.13 | async-start | bytes 6291456 | tf_op jit(solution)/shard_map/reduce_scatter | solution.py:67
  1110.6 88.0 %collective-permute-start.4 = (bf16[1024,2048]{1,0:T(8,128)(2,1)}, bf16[1024,2048]{1,0:T(8,128)(2,1)S(1)}, u32[]{:S(2)}, u32[]{:S(2)}) collective-permute-start(bf16[1024,2048]{1,0:T(8,128)(2,1)} %get-tuple-element.106), channel_id=1, source_target_pairs={{0,6},{2,0},{4,2},{6,4},{1,7},{3,1},{5,3},{7,5},{8,14},{10,8},{12,... | collective-permute-start | bytes 12582920 | tf_op jit(solution)/shard_map/ppermute | solution.py:28
  1170.0 60.6 %collective-permute-start.5 = (bf16[1024,2048]{1,0:T(8,128)(2,1)}, bf16[1024,2048]{1,0:T(8,128)(2,1)S(1)}, u32[]{:S(2)}, u32[]{:S(2)}) collective-permute-start(bf16[1024,2048]{1,0:T(8,128)(2,1)} %collective-permute-done.3), channel_id=1, source_target_pairs={{0,2},{2,4},{4,6},{6,0},{1,3},{3,5},{5,7},{7,1},{8,10},{10,12},{12... | collective-permute-start | bytes 12582920 | tf_op jit(solution)/shard_map/ppermute | solution.py:23
  1200.9 31.9 %copy-start.16 = (bf16[2048,256]{1,0:T(8,128)(2,1)S(1)}, bf16[2048,256]{1,0:T(8,128)(2,1)}, u32[]{:S(2)}) copy-start(bf16[2048,256]{1,0:T(8,128)(2,1)} %param.28) | copy-start | bytes 3145732
  1242.9 54.4 %copy-start.8 = (bf16[2048,256]{1,0:T(8,128)(2,1)S(1)}, bf16[2048,256]{1,0:T(8,128)(2,1)}, u32[]{:S(2)}) copy-start(bf16[2048,256]{1,0:T(8,128)(2,1)} %param.33) | copy-start | bytes 3145732
  1242.9 54.4 %copy-start.33 = (f32[256]{0:T(256)S(1)}, f32[256]{0:T(256)}, u32[]{:S(2)}) copy-start(f32[256]{0:T(256)} %param.29) | copy-start | bytes 3076
  1242.9 93.5 %all-gather.11.cloned.1.call-start = ((), (), s32[]{:S(2)}) async-start(), calls=%async_computation.17 | async-start | bytes 3145728 | tf_op jit(solution)/shard_map/all_gather | solution.py:44
  1303.1 111.0 %reduce-scatter.21.cloned.1.call-start = ((), (), s32[]{:S(2)}) async-start(), calls=%async_computation.18 | async-start | bytes 10485760 | tf_op jit(solution)/shard_map/reduce_scatter | solution.py:50
  1342.5 71.6 %copy-start.30 = (pred[1024]{0:T(1024)(128)(4,1)S(1)}, pred[1024]{0:T(1024)(128)(4,1)}, u32[]{:S(2)}) copy-start(pred[1024]{0:T(1024)(128)(4,1)} %copy-done.29) | copy-start | bytes 3076
  1342.5 403.6 %all-reduce.9.cloned.1.call-start = ((), (), s32[]{:S(2)}) async-start(), calls=%async_computation.20 | async-start | bytes 6291456 | tf_op jit(solution)/shard_map/psum | solution.py:253
  1416.6 13.5 copy-start.9
  1497.0 6.1 copy-start.17
  1497.0 6.1 copy-start.18
  1503.1 73.0 %copy-start.7 = (bf16[4096,256]{1,0:T(8,128)(2,1)S(1)}, bf16[4096,256]{1,0:T(8,128)(2,1)}, u32[]{:S(2)}) copy-start(bf16[4096,256]{1,0:T(8,128)(2,1)} %all-gather.9.cloned.1.call-done) | copy-start | bytes 6291460
  1506.1 79.4 %slice-start = ((s8[16777216]{0:T(1024)(128)(4,1)}), s8[4194304]{0:T(1024)(128)(4,1)S(1)}, s32[]{:S(2)}) async-start(s8[16777216]{0:T(1024)(128)(4,1)} %bitcast.63), calls=%async_computation.21 | async-start | bytes 8388608
  1506.1 79.4 %slice-start.1 = ((s8[16777216]{0:T(1024)(128)(4,1)}), s8[4194304]{0:T(1024)(128)(4,1)S(1)}, s32[]{:S(2)}) async-start(s8[16777216]{0:T(1024)(128)(4,1)} %bitcast.63), calls=%async_computation.22 | async-start | bytes 8388608
  1506.1 79.4 %slice-start.2 = ((s8[16777216]{0:T(1024)(128)(4,1)}), s8[4194304]{0:T(1024)(128)(4,1)S(1)}, s32[]{:S(2)}) async-start(s8[16777216]{0:T(1024)(128)(4,1)} %bitcast.63), calls=%async_computation.23 | async-start | bytes 8388608
  1506.1 79.4 %slice-start.3 = ((s8[16777216]{0:T(1024)(128)(4,1)}), s8[4194304]{0:T(1024)(128)(4,1)S(1)}, s32[]{:S(2)}) async-start(s8[16777216]{0:T(1024)(128)(4,1)} %bitcast.63), calls=%async_computation.24 | async-start | bytes 8388608
  1506.1 79.5 %copy-start.6 = (bf16[4096,256]{1,0:T(8,128)(2,1)S(1)}, bf16[4096,256]{1,0:T(8,128)(2,1)}, u32[]{:S(2)}) copy-start(bf16[4096,256]{1,0:T(8,128)(2,1)} %all-gather.7.cloned.1.call-done) | copy-start | bytes 6291460
  1506.1 70.0 %collective-permute-start.9 = (bf16[1024,1536]{0,1:T(8,128)(2,1)}, bf16[1024,1536]{0,1:T(8,128)(2,1)}, u32[]{:S(2)}, u32[]{:S(2)}) collective-permute-start(bf16[1024,1536]{0,1:T(8,128)(2,1)} %get-tuple-element.108), channel_id=1, source_target_pairs={{0,2},{2,4},{4,6},{6,0},{1,3},{3,5},{5,7},{7,1},{8,10},{10,12},{12... | collective-permute-start | bytes 9437192 | tf_op jit(solution)/shard_map/ppermute | solution.py:23
  1506.2 90.8 %collective-permute-start.10 = (bf16[1024,1536]{0,1:T(8,128)(2,1)}, bf16[1024,1536]{0,1:T(8,128)(2,1)}, u32[]{:S(2)}, u32[]{:S(2)}) collective-permute-start(bf16[1024,1536]{0,1:T(8,128)(2,1)} %get-tuple-element.108), channel_id=1, source_target_pairs={{0,6},{2,0},{4,2},{6,4},{1,7},{3,1},{5,3},{7,5},{8,14},{10,8},{12,... | collective-permute-start | bytes 9437192 | tf_op jit(solution)/shard_map/ppermute | solution.py:28
  1576.1 37.0 %collective-permute-start.11 = (bf16[1024,1536]{0,1:T(8,128)(2,1)}, bf16[1024,1536]{0,1:T(8,128)(2,1)}, u32[]{:S(2)}, u32[]{:S(2)}) collective-permute-start(bf16[1024,1536]{0,1:T(8,128)(2,1)} %collective-permute-done.9), channel_id=1, source_target_pairs={{0,2},{2,4},{4,6},{6,0},{1,3},{3,5},{5,7},{7,1},{8,10},{10,12},{12... | collective-permute-start | bytes 9437192 | tf_op jit(solution)/shard_map/ppermute | solution.py:23
  1585.6 5.5 copy-start.5
  1585.6 5.5 copy-start.12
  1596.9 20.1 %copy-start.11 = (bf16[4096,256]{1,0:T(8,128)(2,1)S(1)}, bf16[4096,256]{1,0:T(8,128)(2,1)}, u32[]{:S(2)}) copy-start(bf16[4096,256]{1,0:T(8,128)(2,1)} %all-gather.5.cloned.1.call-done) | copy-start | bytes 6291460
  1617.0 7.9 copy-start.15
  1624.6 177.2 %reduce-scatter.23.cloned.1.call-start = ((), (), s32[]{:S(2)}) async-start(), calls=%async_computation.19 | async-start | bytes 6291456 | tf_op jit(solution)/shard_map/reduce_scatter | solution.py:67
  1645.4 156.4 %copy-start.3 = (bf16[2048,256]{1,0:T(8,128)(2,1)S(1)}, bf16[2048,256]{1,0:T(8,128)(2,1)}, u32[]{:S(2)}) copy-start(bf16[2048,256]{1,0:T(8,128)(2,1)} %param.17) | copy-start | bytes 3145732
  1645.4 156.4 %copy-start.22 = (f32[2048]{0:T(1024)S(1)}, f32[2048]{0:T(1024)}, u32[]{:S(2)}) copy-start(f32[2048]{0:T(1024)} %copy-done.21) | copy-start | bytes 24580
  1645.5 156.4 %copy-start.24 = (f32[2048]{0:T(1024)S(1)}, f32[2048]{0:T(1024)}, u32[]{:S(2)}) copy-start(f32[2048]{0:T(1024)} %copy-done.23) | copy-start | bytes 24580
  1645.5 156.3 %copy-start.31 = (f32[256]{0:T(256)S(1)}, f32[256]{0:T(256)}, u32[]{:S(2)}) copy-start(f32[256]{0:T(256)} %param.18) | copy-start | bytes 3076
  1746.1 7.3 copy-start.13
  1753.4 87.8 %copy-start.1 = (bf16[256,2048]{1,0:T(8,128)(2,1)S(1)}, bf16[256,2048]{1,0:T(8,128)(2,1)}, u32[]{:S(2)}) copy-start(bf16[256,2048]{1,0:T(8,128)(2,1)} %param.26) | copy-start | bytes 3145732
Sparse Core Ops, SparseCore 0:
  25.2 33.3 all-gather.4
  70.6 181.9 reduce-scatter.8
  350.4 54.0 reduce-scatter.10
  406.0 33.0 all-gather.8
  441.1 33.0 all-gather.6
  476.6 232.3 reduce-scatter.16
  711.6 232.3 reduce-scatter.12
  1110.7 54.1 reduce-scatter.18
  1243.0 54.1 reduce-scatter.14
  1303.2 33.0 all-gather.10
  1342.6 71.4 reduce-scatter.20
  1624.7 121.3 all-reduce.8
  1748.4 53.3 reduce-scatter.22
